TPU v7x, 32 devices: a whole 2x2x4 slice. The times are simulated.
32 devices in a mesh: kpt: 2 (over y), row: 4 (over x, core), col: 4 (over z).
Axes of the slice: x: 2, y: 2, z: 4, core: 2. Of those that a mesh axis runs over, the one named last changes fastest.
Arguments:
- left_blocks: bfloat16 [8, 64, 2, 2, 128, 128], P(('kpt', 'row'), 'col'), parts along dimension 0, may hold values from -0.5 to 0.5
- left_rows: int32 [8, 64, 2], P(('kpt', 'row'), 'col'), parts along dimension 0, may hold values from 0 to 7, as said below
- left_count: int32 [8, 64], P(('kpt', 'row'), 'col'), parts along dimension 0, may hold values from 1 to 2, as said below
- left_level: int32 [8, 64, 2], P(('kpt', 'row'), 'col'), parts along dimension 0, may hold values from 0 to 7
- right_blocks: bfloat16 [2, 64, 4, 4, 2, 128, 128], P('kpt', 'row', 'col'), parts along dimension 0, may hold values from -6 to 6
- right_cols: int32 [2, 64, 4, 4], P('kpt', 'row', 'col'), parts along dimension 0, may hold values from 0 to 15, as said below
- right_count: int32 [2, 64, 4], P('kpt', 'row', 'col'), parts along dimension 0, may hold values from 1 to 4, as said below
- right_level: int32 [2, 64, 4, 4], P('kpt', 'row', 'col'), parts along dimension 0, may hold values from 0 to 7
Outputs:
- product_blocks: bfloat16 [64, 64, 2, 128, 128], P(('kpt', 'row'), 'col'), parts along dimension 0
There are 2 independent parts, one for each index of `kpt`. A program takes and returns all parts, laid end to end along the dimension named above; each array names one. Nothing has to cross between parts.
Inputs may be any that keep to these rules, and one draw needn't show every extreme that they name: `left_rows`: the 2 slots of one row group and block column name distinct block rows. `left_count`: in every row group some block column has all 2 slots live. `right_cols`: the 4 slots of one block row and column group name distinct block columns. `right_count`: in every column group some block row has all 4 slots live.
All inputs are finite; a program needn't handle non-finite values.
Results may differ from a plain program's by a relative error of at most 0.001.
Values may be sent and summed in bfloat16 or wider, within the bound.
A program may use at most 256 MiB of HBM per device.

v0:
```python
import functools

import jax
import jax.numpy as jnp
from jax import lax
from jax.experimental import pallas as pl
from jax.experimental.pallas import tpu as pltpu
from jax.sharding import PartitionSpec as P

GR = 8
LEVEL_CUT = 7
DEAD = -1000
GROUP = 4
MAIN_CUTS = 2
RIGHT_CUTS = 8
VMEM_BYTES = 62 * 1024 * 1024
MESH = pl.DeviceIdType.MESH
FAR = 2.0 ** 17


def variants(slots, n_col, right_slots):
    main, head = slots * 18 // 32, slots * 27 // 32
    middle, rights = slots * 30 // 32, right_slots * 56 // 64
    scale = slots * (n_col - 1) / 96
    found = [
        (main, max(1, int(spill * scale)), head, middle, rights) for spill in (5, 7, 9, 11, 13, 16)
    ]
    found.append((main, max(1, int(24 * scale)), slots, slots, right_slots))
    return found + [(slots, 0, slots, slots, right_slots)]


def ordered(levels, end, union, slots, lane_row):
    ma, per = levels.shape[0], slots // levels.shape[0]
    rows, columns = [], []
    lane = lax.broadcasted_iota(jnp.int32, (per, 128), 1)
    line = lax.broadcasted_iota(jnp.int32, (per, 128), 0)
    for m in range(ma):
        kind = jnp.where(
            levels[m:m + 1] + end >= LEVEL_CUT, 0.0,
            jnp.where(levels[m:m + 1] + union >= LEVEL_CUT, 1.0, 2.0),
        )
        key = jnp.where(lane_row < per, kind * 128.0 + lane_row * ma + m, 1024.0)
        rows.append(key)
        columns.append(jnp.sum(
            jnp.where(lane == line, jnp.broadcast_to(key, (per, 128)), 0.0), axis=1, keepdims=True
        ))
    return rows, columns


def spilled(levels, end, main):
    hits = [
        jnp.where(levels[m:m + 1] + end >= LEVEL_CUT, 1.0, 0.0) for m in range(levels.shape[0])
    ]
    size = jnp.sum(functools.reduce(jnp.add, hits), axis=1, keepdims=True)
    return jnp.maximum(size - main, 0.0)


def placed(live, per, lane, line):
    padded = live if live.shape[1] == 128 else jnp.concatenate(
        [live, jnp.zeros((1, 128 - per), jnp.float32)], axis=1
    )
    wide = jnp.broadcast_to(padded, (per, 128))
    own = jnp.sum(jnp.where(lane == line, wide, 0.0), axis=1, keepdims=True)
    first = jnp.sum(jnp.where(lane < line, wide, 0.0), axis=1, keepdims=True)
    return own, first


def plan_kernel(
    sizes, options, left_level, left_rows, left_count, right_level, right_cols, right_count,
    meta, tiles, perm, choice, tile, send, recv,
):
    n_kpt, n_row, n_col, sets, per, ma, mb = sizes
    slots = per * ma
    kpt, row, col = (lax.axis_index(name) for name in ("kpt", "row", "col"))
    total = n_kpt * n_row * n_col
    me = (kpt * n_row + row) * n_col + col

    def place_of(step):
        other = (me + step) % total
        return {
            "kpt": other // (n_row * n_col), "row": (other // n_col) % n_row, "col": other % n_col
        }

    def copy_of(step):
        return pltpu.make_async_remote_copy(
            src_ref=tile, dst_ref=tiles.at[me], send_sem=send.at[step], recv_sem=recv.at[step],
            device_id=place_of(step), device_id_type=MESH,
        )

    barrier = pltpu.get_barrier_semaphore()

    @pl.loop(1, total)
    def _(step):
        pl.semaphore_signal(barrier, inc=1, device_id=place_of(step), device_id_type=MESH)

    tile[...] = jnp.full(tile.shape, DEAD, jnp.int32)
    live = lax.broadcasted_iota(jnp.int32, (ma, per), 0) < left_count[...]
    levels = jnp.where(live, left_level[...], DEAD)
    tile[:ma, :per] = levels
    rights = []
    for which in range(sets):
        live = lax.broadcasted_iota(jnp.int32, (mb, per), 0) < right_count[which]
        rights.append(jnp.where(live, right_level[which], DEAD))
        tile[ma + which:ma + which + 1, :per] = jnp.max(rights[-1], axis=0, keepdims=True)
        size = jnp.sum(right_count[which].astype(jnp.float32), axis=1, keepdims=True)
        tile[ma + which:ma + which + 1, 127:] = size.astype(jnp.int32)
    tiles[me] = tile[...]
    pl.semaphore_wait(barrier, total - 1)

    @pl.loop(1, total)
    def _(step):
        copy_of(step).start()

    meta[...] = jnp.full(meta.shape, DEAD, jnp.int32)
    meta[:ma, :per] = levels
    meta[ma:2 * ma, :per] = left_rows[...]
    for which in range(sets):
        base = 2 * ma + which * 2 * mb
        meta[base:base + mb, :per] = right_cols[which]
        meta[base + mb:base + 2 * mb, :per] = rights[which]

    @pl.loop(1, total)
    def _(step):
        copy_of(step).wait_recv()

    def at_device(k, r, c):
        return (k * n_row + r) * n_col + c

    def right_max(k, panel, q):
        return tiles[at_device(k, panel % n_row, q), pl.ds(ma + panel // n_row, 1), :]

    def measure_part(k, carry):
        most_end, most_mid, most_spill, most_right = carry
        spills = [zero, zero]
        for panel in range(n_col):
            levels = [
                jnp.concatenate(
                    [tiles[at_device(k, r, panel), pl.ds(m, 1), :] for r in range(n_row)], axis=0
                )
                for m in range(ma)
            ]

            def needed(most):
                hits = [jnp.where(level + most >= LEVEL_CUT, 1.0, 0.0) for level in levels]
                return jnp.sum(functools.reduce(jnp.add, hits), axis=1, keepdims=True)

            rights = [right_max(k, panel, q) for q in range(n_col)]
            for right in rights:
                most_right = jnp.maximum(most_right, right)
            for way, (taken, right) in enumerate(
                ((panel > 0, rights[0]), (panel < n_col - 1, rights[-1]))
            ):
                if taken:
                    wanted = needed(right)
                    most_end = jnp.maximum(most_end, wanted)
                    spills[way] = spills[way] + jnp.maximum(wanted - main, 0.0)
            if panel > 1:
                union = functools.reduce(jnp.maximum, rights[:panel])
                most_mid = jnp.maximum(most_mid, needed(union))
            if panel < n_col - 2:
                union = functools.reduce(jnp.maximum, rights[panel + 1:])
                most_mid = jnp.maximum(most_mid, needed(union))
        most_spill = jnp.maximum(most_spill, jnp.maximum(*spills))
        return most_end, most_mid, most_spill, most_right

    main = options[0][0]
    zero = jnp.zeros((n_row, 1), jnp.float32)
    most_end, most_mid, most_spill, most_right = lax.fori_loop(
        0, n_kpt, measure_part, (zero, zero, zero, jnp.zeros((1, 128), jnp.int32))
    )
    lanes = lax.broadcasted_iota(jnp.int32, (1, 128), 1)
    most_right = jnp.max(
        jnp.where(lanes == 127, most_right, 0).astype(jnp.float32), axis=1, keepdims=True
    )
    index = zero
    for _, spill, head, middle, limit in options[:-1]:
        over = (most_spill > spill) | (most_end > head) | (most_mid > middle)
        index = index + jnp.where(over | (most_right > limit), 1.0, 0.0)
    choice[0] = jnp.max(index).astype(jnp.int32)

    lane_row = lax.broadcasted_iota(jnp.int32, (1, 128), 1).astype(jnp.float32)
    line = lax.broadcasted_iota(jnp.int32, (per, 128), 0).astype(jnp.float32)
    mine = tiles[me, :ma, :]
    for at, up in enumerate((False, True)):
        which = ma + col // n_row
        near = [
            tiles[at_device(kpt, col % n_row, q), pl.ds(which, 1), :] for q in range(n_col)
        ]
        union = jnp.full((1, 128), DEAD, jnp.int32)
        for q in range(n_col):
            beyond = q > col if up else q < col
            union = jnp.maximum(union, jnp.where(beyond, near[q], DEAD))
        rows, columns = ordered(mine, near[-1] if up else near[0], union, slots, lane_row)
        found = jnp.zeros((1, 128), jnp.float32)
        for m in range(ma):
            before = [jnp.where(key < columns[m], 1.0, 0.0) for key in rows]
            rank = jnp.sum(functools.reduce(jnp.add, before), axis=1, keepdims=True)
            hit = jnp.where(rank == lane_row, line * ma + m, 0.0)
            found = found + jnp.sum(hit, axis=0, keepdims=True)
        perm[pl.ds(at, 1), :] = found.astype(jnp.int32)

    for at, up in ((2, False), (3, True)):
        panels = range(n_col - 2, -1, -1) if up else range(1, n_col)
        code, low = jnp.zeros((1, 128), jnp.float32), jnp.zeros((1, 1), jnp.float32)
        for panel in panels:
            levels = tiles[at_device(kpt, row, panel), :ma, :]
            end = right_max(kpt, panel, n_col - 1 if up else 0)
            high = low + spilled(levels, end, main)
            own = up and panel == n_col - 2
            base = (n_col if own else panel) * slots
            inside = (lane_row >= low) & (lane_row < high)
            code = code + jnp.where(inside, base + lane_row - low, 0.0)
            low = high
        perm[pl.ds(at, 1), :] = code.astype(jnp.int32)
    lane = lax.broadcasted_iota(jnp.int32, (per, 128), 1).astype(jnp.float32)
    for which in range(sets):
        live, first = placed(right_count[which].astype(jnp.float32), per, lane, line)
        found = jnp.zeros((1, 128), jnp.float32)
        for n in range(mb):
            hit = jnp.where((first + n == lane) & (live > n), line * mb + n, 0.0)
            found = found + jnp.sum(hit, axis=0, keepdims=True)
        perm[pl.ds(4 + which, 1), :] = found.astype(jnp.int32)

    @pl.loop(1, total)
    def _(step):
        copy_of(step).wait_send()


def order_pairs(sizes, main, kpt, col, tiles, left_meta, right_meta, order):
    n_row, n_col, sets, per, ma, mb, kb_cols = sizes
    slots, high = per * ma, n_col * per
    blocks = GR * kb_cols
    lane_row = lax.broadcasted_iota(jnp.int32, (1, 128), 1).astype(jnp.float32)

    def right_max(panel, q):
        at = (kpt * n_row + panel % n_row) * n_col + q
        return tiles[at, pl.ds(ma + panel // n_row, 1), :]

    lefts = jnp.zeros((2 * ma, 128), jnp.float32)
    rights = jnp.zeros((2 * mb, 128), jnp.float32)
    places = jnp.zeros((8, 128), jnp.float32)
    spots = jnp.zeros((8, 128), jnp.float32)
    thin = lax.broadcasted_iota(jnp.int32, (per, 128), 1).astype(jnp.float32)
    thick = lax.broadcasted_iota(jnp.int32, (per, 128), 0).astype(jnp.float32)
    lows, low = [None] * n_col, jnp.zeros((1, 1), jnp.float32)
    for panel in range(1, n_col):
        lows[panel] = low
        low = low + spilled(left_meta[panel, :ma, :], right_max(panel, 0), main)
    low = jnp.zeros((1, 1), jnp.float32)
    for panel in range(n_col - 2, -1, -1):
        lows[panel] = low if lows[panel] is None else jnp.where(col == 0, lows[panel], low)
        low = low + spilled(left_meta[panel, :ma, :], right_max(panel, n_col - 1), main)
    for panel in range(n_col):
        levels = left_meta[panel, :ma, :]
        down, up = panel > col, panel < col
        end = jnp.where(down, right_max(panel, 0), right_max(panel, n_col - 1))
        union = jnp.full((1, 128), DEAD, jnp.int32)
        for q in range(n_col):
            beyond = down if q < panel else up
            if q != panel:
                union = jnp.maximum(union, jnp.where(beyond, right_max(panel, q), DEAD))
        rows, columns = ordered(levels, end, union, slots, lane_row)
        found = []
        for m in range(ma):
            before = [jnp.where(key < rows[m], 1.0, 0.0) for key in columns]
            rank = jnp.sum(functools.reduce(jnp.add, before), axis=0, keepdims=True)
            own = jnp.where(down | up, rank, lane_row * ma + m) + panel * slots
            far = (down | up) & ((col == 0) | (col == n_col - 1)) & (rank >= main)
            found.append(jnp.where(far, n_col * slots + lows[panel] + rank - main, own))
        found = jnp.concatenate(found + [jnp.zeros((8 - ma, 128), jnp.float32)], axis=0)
        base = 2 * ma + panel // n_row * 2 * mb
        here = (lane_row >= panel * per) & (lane_row < (panel + 1) * per)

        def moved(values):
            values = pltpu.roll(values, panel * per, 1) if panel else values
            return jnp.where(here, values, 0.0)

        lefts = lefts + moved(left_meta[panel, :2 * ma, :].astype(jnp.float32))
        right = right_meta[panel % n_row, base:base + 2 * mb, :].astype(jnp.float32)
        rights = rights + moved(right)
        places = places + moved(found)
        size = jnp.zeros((1, 128), jnp.float32)
        for n in range(mb):
            size = size + jnp.where((right[mb + n:mb + n + 1] > DEAD / 2) & (lane_row < per), 1.0, 0.0)
        live, _ = placed(size, per, thin, thick)
        first = jnp.sum(jnp.where(thick < thin, live, 0.0), axis=0, keepdims=True)
        spots = spots + moved(
            jnp.broadcast_to(jnp.where(lane_row < per, first, 0.0) + panel * per * mb, (8, 128))
        )

    lane = lax.broadcasted_iota(jnp.int32, (high, 128), 1)
    line = lax.broadcasted_iota(jnp.int32, (high, 128), 0)

    def column(values):
        wide = jnp.broadcast_to(values, (high, 128))
        return jnp.sum(jnp.where(lane == line, wide, 0.0), axis=1, keepdims=True)

    keys, key_columns, code_columns, target_columns = [], [], [], []
    for m in range(ma):
        for n in range(mb):
            kept = lefts[m:m + 1] + rights[mb + n:mb + n + 1] >= LEVEL_CUT
            target = lefts[ma + m:ma + m + 1] * kb_cols + rights[n:n + 1]
            spot = lane_row + (m * mb + n) * 128.0
            key = jnp.where(kept, target * 1024.0 + spot, FAR + spot)
            keys.append(jnp.where(lane_row < high, key, 2 * FAR))
            key_columns.append(column(keys[-1]))
            code = places[m:m + 1] * 1024.0 + spots[:1] + n
            code_columns.append(column(jnp.where(kept, code, 0.0)))
            target_columns.append(column(jnp.where(kept, target, 1.0 * blocks)))
    ranks = []
    for mine in key_columns:
        before = [jnp.where(key < mine, 1.0, 0.0) for key in keys]
        ranks.append(jnp.sum(functools.reduce(jnp.add, before), axis=1, keepdims=True))

    def gathered(hits):
        return jnp.sum(functools.reduce(jnp.add, hits), axis=0, keepdims=True)

    def write(at, values):
        order[pl.ds(at, 1), :] = values.astype(jnp.int32)

    lines = -(-high * ma * mb // 128)
    for at in range(lines):
        spot = lane_row + at * 128.0
        for base, columns in ((0, code_columns), (lines, target_columns)):
            write(base + at, gathered([
                jnp.where(rank == spot, values, 0.0) for rank, values in zip(ranks, columns)
            ]))
    bound = (lane_row + 1.0) * (kb_cols * 1024.0)
    write(2 * lines, gathered([jnp.where(mine < bound, 1.0, 0.0) for mine in key_columns]))
    filled = gathered([jnp.where(mine == lane_row, 1.0, 0.0) for mine in target_columns])
    empty = jnp.where((filled < 0.5) & (lane_row < blocks), 1.0, 0.0)
    lane = lax.broadcasted_iota(jnp.int32, (128, 128), 1).astype(jnp.float32)
    line = lax.broadcasted_iota(jnp.int32, (128, 128), 0).astype(jnp.float32)
    wide = jnp.broadcast_to(empty, (128, 128))
    rank = jnp.sum(jnp.where(lane < line, wide, 0.0), axis=1, keepdims=True)
    flag = jnp.sum(jnp.where(lane == line, wide, 0.0), axis=1, keepdims=True)
    write(2 * lines + 1, gathered([jnp.where(rank == lane, line * flag, 0.0)]))
    write(2 * lines + 2, jnp.broadcast_to(jnp.sum(empty, axis=1, keepdims=True), (1, 128)))


def gather_kernel(
    sizes, option, left, right, perm, meta, tiles,
    left_all, right_all, order,
    own_left, own_right, packed_down, packed_up, side, spill_down, spill_up,
    left_meta, right_meta,
    up_send, up_recv, down_send, down_recv, spill_send, spill_recv,
    x_send, x_recv, own_send, own_recv, pass_send, pass_recv,
    lm_send, lm_recv, rm_send, rm_recv, stage_sem, right_sem, left_sem,
):
    n_row, n_col, sets = sizes[:3]
    row = lax.axis_index("row")
    col = lax.axis_index("col")
    n_chip = n_row // 2
    chip, core = row // 2, row % 2
    partner = chip * 2 + 1 - core
    slots = left.shape[0]
    main, spill, head, middle, limit = option

    stages = (
        pltpu.make_async_copy(left, own_left, stage_sem),
        pltpu.make_async_copy(right, own_right, right_sem),
        pltpu.make_async_copy(left, left_all.at[pl.ds(col * slots, slots)], left_sem),
    )
    for copy in stages:
        copy.start()
    barrier = pltpu.get_barrier_semaphore()
    for step in range(1, n_row):
        pl.semaphore_signal(
            barrier, inc=1, device_id={"row": (row + step) % n_row}, device_id_type=MESH
        )
    for step in range(1, n_col):
        pl.semaphore_signal(
            barrier, inc=1, device_id={"col": (col + step) % n_col}, device_id_type=MESH
        )

    bounds = [main * at // MAIN_CUTS for at in range(MAIN_CUTS + 1)]
    cuts = [(low, high, "main") for low, high in zip(bounds, bounds[1:])]
    if head > main:
        cuts.append((main, head, "side"))
    if middle > head:
        cuts.append((head, middle, "rest"))
    bounds = [limit * at // RIGHT_CUTS for at in range(RIGHT_CUTS + 1)]
    right_cuts = [pl.ds(low, high - low) for low, high in zip(bounds, bounds[1:])]

    def left_copy(step, cut, up):
        low, high, kind = cuts[cut]
        panel = col - step if up else col + step
        span = pl.ds(panel * slots + low, high - low)
        target = side.at[span] if kind == "side" else left_all.at[span]
        source = (packed_up if up else packed_down).at[pl.ds(low, high - low)]
        send, recv = (up_send, up_recv) if up else (down_send, down_recv)
        return pltpu.make_async_remote_copy(
            src_ref=source if step == 0 else target, dst_ref=target,
            send_sem=send.at[step, cut], recv_sem=recv.at[step, cut],
            device_id={"col": col + 1 if up else col - 1}, device_id_type=MESH,
        )

    def left_sends(step, cut, up):
        mid = 0 if cuts[cut][2] == "main" else 1
        if up:
            return (col + 1 < n_col - mid) & (col - step >= 0)
        return (col - 1 >= mid) & (col + step < n_col)

    def left_receives(step, cut, up):
        mid = 0 if cuts[cut][2] == "main" else 1
        if up:
            return (col - 1 - step >= 0) & (col < n_col - mid)
        return (col + 1 + step < n_col) & (col >= mid)

    def start_left(step, cut):
        for up in (True, False):
            pl.when(left_sends(step, cut, up))(left_copy(step, cut, up).start)

    def spill_copy(up):
        return pltpu.make_async_remote_copy(
            src_ref=spill_up if up else spill_down,
            dst_ref=left_all.at[pl.ds(n_col * slots, spill)],
            send_sem=spill_send.at[int(up)], recv_sem=spill_recv.at[int(up)],
            device_id={"col": n_col - 1 if up else 0}, device_id_type=MESH,
        )

    def across(step, cut):
        span = right_cuts[cut]
        other = ((chip + step) % n_chip) * 2 + core
        return pltpu.make_async_remote_copy(
            src_ref=right_all.at[:, row, span], dst_ref=right_all.at[:, row, span],
            send_sem=x_send.at[step - 1, cut], recv_sem=x_recv.at[step - 1, cut],
            device_id={"row": other}, device_id_type=MESH,
        )

    def passed(step, cut):
        span = right_cuts[cut]
        panel = ((chip + n_chip - step) % n_chip) * 2 + core
        return pltpu.make_async_remote_copy(
            src_ref=right_all.at[:, panel, span], dst_ref=right_all.at[:, panel, span],
            send_sem=pass_send.at[step - 1, cut], recv_sem=pass_recv.at[step - 1, cut],
            device_id={"row": partner}, device_id_type=MESH,
        )

    own = pltpu.make_async_remote_copy(
        src_ref=right_all.at[:, row, pl.ds(0, limit)],
        dst_ref=right_all.at[:, row, pl.ds(0, limit)],
        send_sem=own_send, recv_sem=own_recv,
        device_id={"row": partner}, device_id_type=MESH,
    )

    stages[0].wait()

    @pl.loop(0, middle)
    def _(at):
        packed_down[at] = own_left[perm[0, at]]
        packed_up[at] = own_left[perm[1, at]]

    left_meta[col] = meta[...]
    right_meta[row] = meta[...]

    def meta_copies():
        for step in range(1, n_col):
            yield pltpu.make_async_remote_copy(
                src_ref=meta, dst_ref=left_meta.at[col],
                send_sem=lm_send.at[step - 1], recv_sem=lm_recv.at[step - 1],
                device_id={"col": (col + step) % n_col}, device_id_type=MESH,
            )
        for step in range(1, n_row):
            yield pltpu.make_async_remote_copy(
                src_ref=meta, dst_ref=right_meta.at[row],
                send_sem=rm_send.at[step - 1], recv_sem=rm_recv.at[step - 1],
                device_id={"row": (row + step) % n_row}, device_id_type=MESH,
            )

    pl.semaphore_wait(barrier, n_row + n_col - 2)
    for copy in meta_copies():
        copy.start()
    for cut in range(len(cuts)):
        if cuts[cut][2] != "rest":
            start_left(0, cut)

    stages[1].wait()
    for which in range(sets):
        @pl.loop(0, limit)
        def _(at):
            right_all[which, row, at] = own_right[which, perm[4 + which, at]]

    for step in range(1, n_chip):
        for cut in range(RIGHT_CUTS):
            across(step, cut).start()
    own.start()
    if spill:
        @pl.loop(main, head)
        def _(at):
            side[col * slots + at] = packed_down[at]
            side[n_col * slots + at] = packed_up[at]

    def take_left(step, cut):
        for up in (True, False):
            pl.when(left_receives(step, cut, up))(left_copy(step, cut, up).wait_recv)
            if step + 1 < n_col - 1:
                pl.when(left_sends(step + 1, cut, up))(left_copy(step + 1, cut, up).start)

    def take_right(step, cut):
        across(step, cut).wait_recv()
        passed(step, cut).start()

    def take_order():
        for copy in meta_copies():
            copy.wait()
        order_pairs(
            sizes, main, lax.axis_index("kpt"), col, tiles, left_meta, right_meta, order
        )

    def send_spill():
        for up in (False, True):
            target, line = (spill_up, 3) if up else (spill_down, 2)

            @pl.when(col == (n_col - 2 if up else 1))
            def _():
                @pl.loop(0, spill)
                def _(at):
                    target[at] = side[perm[line, at] + main]

                spill_copy(up).start()

    heads = (n_col - 2) * head
    jobs = [(7, take_order)]
    if spill:
        jobs.append((heads + 0.02, send_spill))
    for cut, (low, high, kind) in enumerate(cuts):
        if kind == "rest":
            jobs.append(((n_col - 3) * head + 0.03, functools.partial(start_left, 0, cut)))
        for step in range(n_col - 1 if kind == "main" else n_col - 2):
            when = step * head + high
            if kind == "rest":
                when = heads + (step + 1) * (high - low) + 0.04
            jobs.append((when, functools.partial(take_left, step, cut)))
    for step in range(1, n_chip):
        for cut in range(RIGHT_CUTS):
            when = ((step - 1) * RIGHT_CUTS + cut + 1) * limit * sets / RIGHT_CUTS + 0.5
            jobs.append((when, functools.partial(take_right, step, cut)))
    for _, job in sorted(jobs, key=lambda entry: entry[0]):
        job()

    stages[2].wait()
    if head > main:
        for step in range(1, n_col):
            for panel, there in (
                (col - step, (col - step >= 0) & (col < n_col - 1)),
                (col + step, (col + step < n_col) & (col > 0)),
            ):
                @pl.when(there)
                def _():
                    @pl.loop(main, head)
                    def _(at):
                        left_all[panel * slots + at] = side[panel * slots + at]

    if spill:
        for up in (False, True):
            pl.when(col == (n_col - 1 if up else 0))(spill_copy(up).wait_recv)
            pl.when(col == (n_col - 2 if up else 1))(spill_copy(up).wait_send)
    own.wait()
    for step in range(1, n_chip):
        for cut in range(RIGHT_CUTS):
            across(step, cut).wait_send()
            passed(step, cut).wait()
    for cut, entry in enumerate(cuts):
        for step in range(n_col - 1 if entry[2] == "main" else n_col - 2):
            for up in (True, False):
                pl.when(left_sends(step, cut, up))(left_copy(step, cut, up).wait_send)


def product_kernel(sizes, left, right, order, out, stage, partial, out_sem):
    n_row, n_col, sets, per, ma, mb, kb_cols = sizes
    blocks = GR * kb_cols
    lines = -(-n_col * per * ma * mb // 128)
    width = stage.shape[2]
    empty = jnp.zeros(stage.shape[1:], stage.dtype)

    @pl.loop(0, order[2 * lines + 2, 0])
    def _(at):
        stage[order[2 * lines + 1, at]] = empty

    def out_copy(line):
        span = pl.ds(line * kb_cols, kb_cols)
        return pltpu.make_async_copy(stage.at[span], out.at[span], out_sem.at[line])

    count = order[2 * lines, GR - 1]

    def group(at, carry):
        line, last = carry
        codes, targets, done = [], [], []
        for lane in range(GROUP):
            spot = at * GROUP + lane
            codes.append(order[spot // 128, spot % 128])
            targets.append(order[lines + spot // 128, spot % 128])
        for code in codes:
            block = left[code // 1024]
            wide = jnp.concatenate([block[:width], block[width:]], axis=1)
            other = right[code % 1024]
            real, imag = other[:width], other[width:]
            matrix = jnp.concatenate(
                [jnp.concatenate([real, imag], axis=1), jnp.concatenate([-imag, real], axis=1)],
                axis=0,
            )
            done.append(jnp.dot(wide, matrix, preferred_element_type=jnp.float32))
        held = partial[...]
        for target, product in zip(targets, done):
            held = jnp.where(target == last, held, 0.0) + product
            value = held.astype(stage.dtype)
            stage[target, :width] = value[:, :width]
            stage[target, width:] = value[:, width:]
            last = target
        partial[...] = held
        ready = (line < GR) & (at * GROUP >= order[2 * lines, jnp.minimum(line, GR - 1)])
        pl.when(ready)(lambda: out_copy(line).start())
        return line + jnp.where(ready, 1, 0), last

    partial[...] = jnp.zeros(partial.shape, partial.dtype)
    line, _ = lax.fori_loop(
        0, (count + GROUP - 1) // GROUP, group, (jnp.int32(0), jnp.int32(-1))
    )

    @pl.loop(line, GR)
    def _(line):
        out_copy(line).start()

    @pl.loop(0, GR)
    def _(line):
        out_copy(line).wait()


def body(
    n_kpt, n_row, n_col, left_blocks, left_rows, left_count, left_level,
    right_blocks, right_cols, right_count, right_level,
):
    _, per, ma, _, width, _ = left_blocks.shape
    sets, right_per, _, mb = right_blocks.shape[:4]
    assert right_per == per and sets * n_row == n_col and n_row % 2 == 0 and sets <= 2
    blocks = GR * (n_row * sets * per // n_col)
    assert n_col * per <= 128 and per * ma <= 128 and blocks <= 128 and ma * mb <= 8
    slots = per * ma
    left = left_blocks.reshape(slots, 2 * width, width)
    right = right_blocks.reshape(sets, per * mb, 2 * width, width)
    any_space = pl.BlockSpec(memory_space=pl.ANY)
    vmem = pl.BlockSpec(memory_space=pltpu.VMEM)
    smem = pl.BlockSpec(memory_space=pltpu.SMEM)
    dma = pltpu.SemaphoreType.DMA
    n_chip = n_row // 2
    total = n_kpt * n_row * n_col
    options = variants(slots, n_col, per * mb)
    sizes = (n_row, n_col, sets, per, ma, mb, n_row * sets * per // n_col)
    tile_rows = -(-(ma + sets) // 4) * 4
    meta_rows = -(-(2 * ma + 2 * mb * sets) // 8) * 8
    lines = -(-n_col * per * ma * mb // 128)
    order_rows = -(-(2 * lines + 3) // 8) * 8
    meta, tiles, perm, choice = pl.pallas_call(
        functools.partial(plan_kernel, (n_kpt,) + sizes[:-1], options),
        out_shape=(
            jax.ShapeDtypeStruct((meta_rows, 128), jnp.int32),
            jax.ShapeDtypeStruct((total, tile_rows, 128), jnp.int32),
            jax.ShapeDtypeStruct((8, 128), jnp.int32),
            jax.ShapeDtypeStruct((1,), jnp.int32),
        ),
        in_specs=[vmem] * 6,
        out_specs=(vmem, vmem, vmem, smem),
        scratch_shapes=[pltpu.VMEM((tile_rows, 128), jnp.int32), dma((total,)), dma((total,))],
        compiler_params=pltpu.CompilerParams(collective_id=0, has_side_effects=True),
        name="plan",
    )(
        left_level[0].T, left_rows[0].T, left_count,
        right_level[:, :, 0].transpose(0, 2, 1), right_cols[:, :, 0].transpose(0, 2, 1),
        right_count.transpose(0, 2, 1),
    )

    kb_cols = sizes[-1]
    right_shape = (sets, n_row) + right.shape[1:]
    most = n_col * left.size + n_row * right.size + 24 * left.size // slots
    limit = VMEM_BYTES - most * left.dtype.itemsize

    def run(at, left, right, perm, meta, tiles):
        cuts, spill = MAIN_CUTS + 2, max(options[at][1], 1)
        left_all, right_all, order = pl.pallas_call(
            functools.partial(gather_kernel, sizes, options[at]),
            out_shape=(
                pltpu.VMEM((n_col * slots + options[at][1],) + left.shape[1:], left.dtype),
                pltpu.VMEM(right_shape, right.dtype),
                jax.ShapeDtypeStruct((order_rows, 128), jnp.int32),
            ),
            in_specs=[any_space, any_space, smem, vmem, vmem],
            out_specs=(vmem, vmem, vmem),
            scratch_shapes=[
                pltpu.VMEM(left.shape, left.dtype),
                pltpu.VMEM(right.shape, right.dtype),
                *[pltpu.VMEM(left.shape, left.dtype)] * 2,
                pltpu.VMEM(((n_col + 1) * slots,) + left.shape[1:], left.dtype),
                *[pltpu.VMEM((spill,) + left.shape[1:], left.dtype)] * 2,
                pltpu.VMEM((n_col, meta_rows, 128), jnp.int32),
                pltpu.VMEM((n_row, meta_rows, 128), jnp.int32),
                *[dma((n_col - 1, cuts))] * 4,
                *[dma((2,))] * 2,
                *[dma((n_chip - 1, RIGHT_CUTS))] * 2,
                *[dma] * 2,
                *[dma((n_chip - 1, RIGHT_CUTS))] * 2,
                *[dma((n_col - 1,))] * 2,
                *[dma((n_row - 1,))] * 2,
                *[dma] * 3,
            ],
            compiler_params=pltpu.CompilerParams(
                collective_id=1 + at, has_side_effects=True, vmem_limit_bytes=limit
            ),
            name=f"gather_panels_{at}",
        )(left, right, perm, meta, tiles)
        return pl.pallas_call(
            functools.partial(product_kernel, sizes),
            out_shape=jax.ShapeDtypeStruct((blocks, 2 * width, width), jnp.bfloat16),
            in_specs=[vmem, vmem, smem],
            out_specs=any_space,
            scratch_shapes=[
                pltpu.VMEM((blocks + 1, 2 * width, width), jnp.bfloat16),
                pltpu.VMEM((width, 2 * width), jnp.float32),
                dma((GR,)),
            ],
            compiler_params=pltpu.CompilerParams(vmem_limit_bytes=limit),
            name="pair_products",
        )(
            pltpu.with_memory_space_constraint(
                left_all, pltpu.VMEM
            ),
            pltpu.with_memory_space_constraint(
                right_all.reshape((-1,) + right.shape[2:]), pltpu.VMEM
            ),
            order,
        )

    out = lax.switch(
        choice[0], [functools.partial(run, at) for at in range(len(options))],
        left, right, perm, meta, tiles,
    )
    return out.reshape(GR, kb_cols, 2, width, width)


def solution(mesh):
    in_specs = (
        P(("kpt", "row"), "col", None, None, None, None),
        P(("kpt", "row"), "col", None),
        P(("kpt", "row"), "col"),
        P(("kpt", "row"), "col", None),
        P("kpt", "row", "col", None, None, None, None),
        P("kpt", "row", "col", None),
        P("kpt", "row", "col"),
        P("kpt", "row", "col", None),
    )
    out_specs = P(("kpt", "row"), "col", None, None, None)
    return jax.shard_map(
        functools.partial(body, mesh.shape["kpt"], mesh.shape["row"], mesh.shape["col"]),
        mesh=mesh, in_specs=in_specs, out_specs=out_specs, check_vma=False,
    )
```

profile of v0, /device:TPU:0, one launch (start us, length us, event | category | flops | bytes accessed | tf_op | source)
XLA Modules:
  0.0 122.4 jit_solution(7795718348494577100)
XLA Ops:
  0.0 12.6 %plan.1 = (s32[16,128]{1,0:T(8,128)S(1)}, s32[32,4,128]{2,1,0:T(4,128)S(1)}, s32[8,128]{1,0:T(8,128)S(1)}, s32[1]{0:T(128)}) custom-call(s32[2,16]{1,0:T(2,128)} %bitcast.66, s32[2,16]{1,0:T(2,128)} %bitcast.67, s32[1,16]{1,0:T(1,128)} %left_count.1, s32[1,4,16]{2,1,0:T(4,128)} %bitcast.64, s32[1,4,16]{2,1,0:T(4,128)} %bitcast.65, s32[1,1,16]{2,1,0:T(1,128)} %bitcast.68), custom_call_target="tpu_custom_call" | custom-call | tf_op jit(solution)/shard_map/plan/pallas_call | solution.py:654
  13.2 109.2 %conditional.1 = (bf16[8,16,2,128,128]{4,3,2,1,0:T(8,128)(2,1)}) conditional(s32[]{:T(128)} %bitcast.25, (bf16[32,256,128]{2,1,0:T(8,128)(2,1)}, bf16[1,64,256,128]{3,2,1,0:T(8,128)(2,1)}, s32[8,128]{1,0:T(8,128)S(1)}, s32[16,128]{1,0:T(8,128)S(1)}, s32[32,4,128]{2,1,0:T(4,128)S(1)}) %tuple.62, ...), branch_computations={%region_0.0_spmd, %region_1.0_spmd, %region_2.0_spmd, %region_3.0_... | conditional | bytes 8 | solution.py:733
  13.2 97.3 %gather_panels_2.1 = (bf16[137,256,128]{2,1,0:T(8,128)(2,1)S(1)}, bf16[1,4,64,256,128]{4,3,2,1,0:T(8,128)(2,1)S(1)}, s32[16,128]{1,0:T(8,128)}) custom-call(bf16[32,256,128]{2,1,0:T(8,128)(2,1)} %get-tuple-element.111.left, bf16[1,64,256,128]{3,2,1,0:T(8,128)(2,1)} %get-tuple-element.112.right, s32[8,128]{1,0:T(8,128)S(1)} %get-tuple-element.113.perm, ...), custom_call_target="tpu_custom_call" | custom-call | tf_op jit(solution)/shard_map/cond/branch_2_fun/gather_panels_2/pallas_call | solution.py:680
  110.5 11.9 %pair_products.10 = bf16[128,256,128]{2,1,0:T(8,128)(2,1)} custom-call(bf16[137,256,128]{2,1,0:T(8,128)(2,1)S(1)} %get-tuple-element.116.left, bf16[256,256,128]{2,1,0:T(8,128)(2,1)S(1)} %bitcast.34, s32[16,128]{1,0:T(8,128)} %get-tuple-element.118.order), custom_call_target="tpu_custom_call" | custom-call | tf_op jit(solution)/shard_map/cond/branch_2_fun/pair_products/pallas_call | solution.py:711
where the time goes:
time: 123 us; the launch traced here: 122 us
  Pallas kernels  122 us (99%)
    pallas_call x1, Pallas kernels, run(): pl.pallas_call(functools.partial(gather_kernel, sizes, options[at]), out_...  97.3 us
    pallas_call x1, Pallas kernels, body(): pl.pallas_call(functools.partial(plan_kernel, (n_kpt,) + sizes[:-1], opti...  12.6 us
    pallas_call x1, Pallas kernels, run(): pl.pallas_call(functools.partial(product_kernel, sizes), out_shape=jax.Sh...  11.9 us

commit v1 on v0

--- a/solution.py
+++ b/solution.py
@@ -10,7 +10,7 @@
 GR = 8
 LEVEL_CUT = 7
 DEAD = -1000
-GROUP = 4
+GROUP = 24
 MAIN_CUTS = 2
 RIGHT_CUTS = 8
 VMEM_BYTES = 62 * 1024 * 1024
@@ -66,8 +66,10 @@
 
 
 def plan_kernel(
-    sizes, options, left_level, left_rows, left_count, right_level, right_cols, right_count,
-    meta, tiles, perm, choice, tile, send, recv,
+    sizes, options, left,
+    left_level, left_rows, left_count, right_level, right_cols, right_count,
+    own_left, left_meta, right_meta, tiles, perm, choice,
+    tile, meta, send, recv, lm_send, lm_recv, rm_send, rm_recv, left_sem,
 ):
     n_kpt, n_row, n_col, sets, per, ma, mb = sizes
     slots = per * ma
@@ -93,6 +95,11 @@
     def _(step):
         pl.semaphore_signal(barrier, inc=1, device_id=place_of(step), device_id_type=MESH)
 
+    stages = (
+        pltpu.make_async_copy(left, own_left, left_sem),
+    )
+    for copy in stages:
+        copy.start()
     tile[...] = jnp.full(tile.shape, DEAD, jnp.int32)
     live = lax.broadcasted_iota(jnp.int32, (ma, per), 0) < left_count[...]
     levels = jnp.where(live, left_level[...], DEAD)
@@ -105,12 +112,6 @@
         size = jnp.sum(right_count[which].astype(jnp.float32), axis=1, keepdims=True)
         tile[ma + which:ma + which + 1, 127:] = size.astype(jnp.int32)
     tiles[me] = tile[...]
-    pl.semaphore_wait(barrier, total - 1)
-
-    @pl.loop(1, total)
-    def _(step):
-        copy_of(step).start()
-
     meta[...] = jnp.full(meta.shape, DEAD, jnp.int32)
     meta[:ma, :per] = levels
     meta[ma:2 * ma, :per] = left_rows[...]
@@ -118,6 +119,30 @@
         base = 2 * ma + which * 2 * mb
         meta[base:base + mb, :per] = right_cols[which]
         meta[base + mb:base + 2 * mb, :per] = rights[which]
+    left_meta[col] = meta[...]
+    right_meta[row] = meta[...]
+    pl.semaphore_wait(barrier, total - 1)
+
+    @pl.loop(1, total)
+    def _(step):
+        copy_of(step).start()
+
+    def meta_copies():
+        for step in range(1, n_col):
+            yield pltpu.make_async_remote_copy(
+                src_ref=meta, dst_ref=left_meta.at[col],
+                send_sem=lm_send.at[step - 1], recv_sem=lm_recv.at[step - 1],
+                device_id={"col": (col + step) % n_col}, device_id_type=MESH,
+            )
+        for step in range(1, n_row):
+            yield pltpu.make_async_remote_copy(
+                src_ref=meta, dst_ref=right_meta.at[row],
+                send_sem=rm_send.at[step - 1], recv_sem=rm_recv.at[step - 1],
+                device_id={"row": (row + step) % n_row}, device_id_type=MESH,
+            )
+
+    for copy in meta_copies():
+        copy.start()
 
     @pl.loop(1, total)
     def _(step):
@@ -220,6 +245,11 @@
             hit = jnp.where((first + n == lane) & (live > n), line * mb + n, 0.0)
             found = found + jnp.sum(hit, axis=0, keepdims=True)
         perm[pl.ds(4 + which, 1), :] = found.astype(jnp.int32)
+
+    for copy in meta_copies():
+        copy.wait()
+    for copy in stages:
+        copy.wait()
 
     @pl.loop(1, total)
     def _(step):
@@ -334,18 +364,19 @@
     wide = jnp.broadcast_to(empty, (128, 128))
     rank = jnp.sum(jnp.where(lane < line, wide, 0.0), axis=1, keepdims=True)
     flag = jnp.sum(jnp.where(lane == line, wide, 0.0), axis=1, keepdims=True)
-    write(2 * lines + 1, gathered([jnp.where(rank == lane, line * flag, 0.0)]))
-    write(2 * lines + 2, jnp.broadcast_to(jnp.sum(empty, axis=1, keepdims=True), (1, 128)))
+    size = jnp.broadcast_to(jnp.sum(empty, axis=1, keepdims=True), (1, 128))
+    listed = gathered([jnp.where(rank == lane, line * flag, 0.0)])
+    write(2 * lines + 1, jnp.where(lane_row < size, listed, 1.0 * blocks))
+    write(2 * lines + 2, size)
 
 
 def gather_kernel(
-    sizes, option, left, right, perm, meta, tiles,
+    sizes, option, left, own_left, right, perm, left_meta, right_meta, tiles,
     left_all, right_all, order,
-    own_left, own_right, packed_down, packed_up, side, spill_down, spill_up,
-    left_meta, right_meta,
+    own_right, packed_down, packed_up, side, spill_down, spill_up,
     up_send, up_recv, down_send, down_recv, spill_send, spill_recv,
     x_send, x_recv, own_send, own_recv, pass_send, pass_recv,
-    lm_send, lm_recv, rm_send, rm_recv, stage_sem, right_sem, left_sem,
+    left_sem, right_sem,
 ):
     n_row, n_col, sets = sizes[:3]
     row = lax.axis_index("row")
@@ -356,22 +387,18 @@
     slots = left.shape[0]
     main, spill, head, middle, limit = option
 
-    stages = (
-        pltpu.make_async_copy(left, own_left, stage_sem),
-        pltpu.make_async_copy(right, own_right, right_sem),
-        pltpu.make_async_copy(left, left_all.at[pl.ds(col * slots, slots)], left_sem),
-    )
-    for copy in stages:
-        copy.start()
     barrier = pltpu.get_barrier_semaphore()
-    for step in range(1, n_row):
-        pl.semaphore_signal(
-            barrier, inc=1, device_id={"row": (row + step) % n_row}, device_id_type=MESH
-        )
-    for step in range(1, n_col):
-        pl.semaphore_signal(
-            barrier, inc=1, device_id={"col": (col + step) % n_col}, device_id_type=MESH
-        )
+    for there, step in ((col > 0, -1), (col + 1 < n_col, 1)):
+        @pl.when(there)
+        def _():
+            pl.semaphore_signal(
+                barrier, inc=1, device_id={"col": col + step}, device_id_type=MESH
+            )
+    others = [partner] + [((chip + step) % n_chip) * 2 + core for step in range(1, n_chip)]
+    for other in others:
+        pl.semaphore_signal(barrier, inc=1, device_id={"row": other}, device_id_type=MESH)
+    kept = pltpu.make_async_copy(left, left_all.at[pl.ds(col * slots, slots)], left_sem)
+    kept.start()
 
     bounds = [main * at // MAIN_CUTS for at in range(MAIN_CUTS + 1)]
     cuts = [(low, high, "main") for low, high in zip(bounds, bounds[1:])]
@@ -444,38 +471,25 @@
         device_id={"row": partner}, device_id_type=MESH,
     )
 
-    stages[0].wait()
-
-    @pl.loop(0, middle)
-    def _(at):
-        packed_down[at] = own_left[perm[0, at]]
-        packed_up[at] = own_left[perm[1, at]]
-
-    left_meta[col] = meta[...]
-    right_meta[row] = meta[...]
-
-    def meta_copies():
-        for step in range(1, n_col):
-            yield pltpu.make_async_remote_copy(
-                src_ref=meta, dst_ref=left_meta.at[col],
-                send_sem=lm_send.at[step - 1], recv_sem=lm_recv.at[step - 1],
-                device_id={"col": (col + step) % n_col}, device_id_type=MESH,
-            )
-        for step in range(1, n_row):
-            yield pltpu.make_async_remote_copy(
-                src_ref=meta, dst_ref=right_meta.at[row],
-                send_sem=rm_send.at[step - 1], recv_sem=rm_recv.at[step - 1],
-                device_id={"row": (row + step) % n_row}, device_id_type=MESH,
-            )
-
-    pl.semaphore_wait(barrier, n_row + n_col - 2)
-    for copy in meta_copies():
-        copy.start()
-    for cut in range(len(cuts)):
+    def pack_left(low, high):
+        @pl.loop(low, high)
+        def _(at):
+            packed_down[at] = own_left[perm[0, at]]
+            packed_up[at] = own_left[perm[1, at]]
+
+    pack_left(*cuts[0][:2])
+    pl.semaphore_wait(
+        barrier, len(others) + jnp.where(col > 0, 1, 0) + jnp.where(col + 1 < n_col, 1, 0)
+    )
+    start_left(0, 0)
+    staged = pltpu.make_async_copy(right, own_right, right_sem)
+    staged.start()
+    pack_left(cuts[0][1], middle)
+    for cut in range(1, len(cuts)):
         if cuts[cut][2] != "rest":
             start_left(0, cut)
 
-    stages[1].wait()
+    staged.wait()
     for which in range(sets):
         @pl.loop(0, limit)
         def _(at):
@@ -502,8 +516,6 @@
         passed(step, cut).start()
 
     def take_order():
-        for copy in meta_copies():
-            copy.wait()
         order_pairs(
             sizes, main, lax.axis_index("kpt"), col, tiles, left_meta, right_meta, order
         )
@@ -539,7 +551,7 @@
     for _, job in sorted(jobs, key=lambda entry: entry[0]):
         job()
 
-    stages[2].wait()
+    kept.wait()
     if head > main:
         for step in range(1, n_col):
             for panel, there in (
@@ -574,9 +586,10 @@
     width = stage.shape[2]
     empty = jnp.zeros(stage.shape[1:], stage.dtype)
 
-    @pl.loop(0, order[2 * lines + 2, 0])
+    @pl.loop(0, (order[2 * lines + 2, 0] + 3) // 4)
     def _(at):
-        stage[order[2 * lines + 1, at]] = empty
+        for lane in range(4):
+            stage[order[2 * lines + 1, at * 4 + lane]] = empty
 
     def out_copy(line):
         span = pl.ds(line * kb_cols, kb_cols)
@@ -609,9 +622,11 @@
             stage[target, width:] = value[:, width:]
             last = target
         partial[...] = held
-        ready = (line < GR) & (at * GROUP >= order[2 * lines, jnp.minimum(line, GR - 1)])
-        pl.when(ready)(lambda: out_copy(line).start())
-        return line + jnp.where(ready, 1, 0), last
+        for _ in range(1 + GROUP // 12):
+            ready = (line < GR) & (at * GROUP >= order[2 * lines, jnp.minimum(line, GR - 1)])
+            pl.when(ready)(out_copy(jnp.minimum(line, GR - 1)).start)
+            line = line + jnp.where(ready, 1, 0)
+        return line, last
 
     partial[...] = jnp.zeros(partial.shape, partial.dtype)
     line, _ = lax.fori_loop(
@@ -651,31 +666,40 @@
     meta_rows = -(-(2 * ma + 2 * mb * sets) // 8) * 8
     lines = -(-n_col * per * ma * mb // 128)
     order_rows = -(-(2 * lines + 3) // 8) * 8
-    meta, tiles, perm, choice = pl.pallas_call(
+    own_left, left_meta, right_meta, tiles, perm, choice = pl.pallas_call(
         functools.partial(plan_kernel, (n_kpt,) + sizes[:-1], options),
         out_shape=(
-            jax.ShapeDtypeStruct((meta_rows, 128), jnp.int32),
+            pltpu.VMEM(left.shape, left.dtype),
+            jax.ShapeDtypeStruct((n_col, meta_rows, 128), jnp.int32),
+            jax.ShapeDtypeStruct((n_row, meta_rows, 128), jnp.int32),
             jax.ShapeDtypeStruct((total, tile_rows, 128), jnp.int32),
             jax.ShapeDtypeStruct((8, 128), jnp.int32),
             jax.ShapeDtypeStruct((1,), jnp.int32),
         ),
-        in_specs=[vmem] * 6,
-        out_specs=(vmem, vmem, vmem, smem),
-        scratch_shapes=[pltpu.VMEM((tile_rows, 128), jnp.int32), dma((total,)), dma((total,))],
+        in_specs=[any_space] + [vmem] * 6,
+        out_specs=(vmem,) * 5 + (smem,),
+        scratch_shapes=[
+            pltpu.VMEM((tile_rows, 128), jnp.int32),
+            pltpu.VMEM((meta_rows, 128), jnp.int32),
+            *[dma((total,))] * 2,
+            *[dma((n_col - 1,))] * 2,
+            *[dma((n_row - 1,))] * 2,
+            dma,
+        ],
         compiler_params=pltpu.CompilerParams(collective_id=0, has_side_effects=True),
         name="plan",
     )(
-        left_level[0].T, left_rows[0].T, left_count,
+        left, left_level[0].T, left_rows[0].T, left_count,
         right_level[:, :, 0].transpose(0, 2, 1), right_cols[:, :, 0].transpose(0, 2, 1),
         right_count.transpose(0, 2, 1),
     )
 
     kb_cols = sizes[-1]
     right_shape = (sets, n_row) + right.shape[1:]
-    most = n_col * left.size + n_row * right.size + 24 * left.size // slots
+    most = (n_col + 1) * left.size + n_row * right.size + 24 * left.size // slots
     limit = VMEM_BYTES - most * left.dtype.itemsize
 
-    def run(at, left, right, perm, meta, tiles):
+    def run(at, left, own_left, right, perm, left_meta, right_meta, tiles):
         cuts, spill = MAIN_CUTS + 2, max(options[at][1], 1)
         left_all, right_all, order = pl.pallas_call(
             functools.partial(gather_kernel, sizes, options[at]),
@@ -684,30 +708,28 @@
                 pltpu.VMEM(right_shape, right.dtype),
                 jax.ShapeDtypeStruct((order_rows, 128), jnp.int32),
             ),
-            in_specs=[any_space, any_space, smem, vmem, vmem],
+            in_specs=[any_space, vmem, any_space, smem, vmem, vmem, vmem],
             out_specs=(vmem, vmem, vmem),
             scratch_shapes=[
-                pltpu.VMEM(left.shape, left.dtype),
                 pltpu.VMEM(right.shape, right.dtype),
                 *[pltpu.VMEM(left.shape, left.dtype)] * 2,
                 pltpu.VMEM(((n_col + 1) * slots,) + left.shape[1:], left.dtype),
                 *[pltpu.VMEM((spill,) + left.shape[1:], left.dtype)] * 2,
-                pltpu.VMEM((n_col, meta_rows, 128), jnp.int32),
-                pltpu.VMEM((n_row, meta_rows, 128), jnp.int32),
                 *[dma((n_col - 1, cuts))] * 4,
                 *[dma((2,))] * 2,
                 *[dma((n_chip - 1, RIGHT_CUTS))] * 2,
                 *[dma] * 2,
                 *[dma((n_chip - 1, RIGHT_CUTS))] * 2,
-                *[dma((n_col - 1,))] * 2,
-                *[dma((n_row - 1,))] * 2,
-                *[dma] * 3,
+                *[dma] * 2,
             ],
             compiler_params=pltpu.CompilerParams(
                 collective_id=1 + at, has_side_effects=True, vmem_limit_bytes=limit
             ),
             name=f"gather_panels_{at}",
-        )(left, right, perm, meta, tiles)
+        )(
+            left, pltpu.with_memory_space_constraint(own_left, pltpu.VMEM),
+            right, perm, left_meta, right_meta, tiles,
+        )
         return pl.pallas_call(
             functools.partial(product_kernel, sizes),
             out_shape=jax.ShapeDtypeStruct((blocks, 2 * width, width), jnp.bfloat16),
@@ -732,7 +754,7 @@
 
     out = lax.switch(
         choice[0], [functools.partial(run, at) for at in range(len(options))],
-        left, right, perm, meta, tiles,
+        left, own_left, right, perm, left_meta, right_meta, tiles,
     )
     return out.reshape(GR, kb_cols, 2, width, width)
 

time: 123 us -> 119 us (0.967)
  Pallas kernels: 122 us -> 117 us
    pallas_call x1, Pallas kernels: 11.9 us -> 7.35 us  [run(): pl.pallas_call(functools.partial(product_kernel, sizes), out_shape=jax.Sh...]
where the time goes in v1:
time: 119 us
  Pallas kernels  117 us (98%)
    pallas_call x1, Pallas kernels, run(): pl.pallas_call(functools.partial(gather_kernel, sizes, options[at]), out_...  96.8 us
    pallas_call x1, Pallas kernels, body(): pl.pallas_call(functools.partial(plan_kernel, (n_kpt,) + sizes[:-1], opti...  13.2 us
    pallas_call x1, Pallas kernels, run(): pl.pallas_call(functools.partial(product_kernel, sizes), out_shape=jax.Sh...  7.35 us

profile of v1, /device:TPU:0, one launch (start us, length us, event | category | flops | bytes accessed | tf_op | source)
XLA Modules:
  0.0 118.5 jit_solution(5612162275180278636)
XLA Ops:
  0.0 13.2 %plan.1 = (bf16[32,256,128]{2,1,0:T(8,128)(2,1)S(1)}, s32[4,16,128]{2,1,0:T(8,128)S(1)}, s32[4,16,128]{2,1,0:T(8,128)S(1)}, s32[32,4,128]{2,1,0:T(4,128)S(1)}, s32[8,128]{1,0:T(8,128)S(1)}, /*index=5*/s32[1]{0:T(128)}) custom-call(bf16[32,256,128]{2,1,0:T(8,128)(2,1)} %bitcast.48, s32[2,16]{1,0:T(2,128)} %bitcast.67, s32[2,16]{1,0:T(2,128)} %bitcast.68, ...), custom_call_target="tpu_custom_call" | custom-call | tf_op jit(solution)/shard_map/plan/pallas_call | solution.py:669
  13.9 104.4 %conditional.1 = (bf16[8,16,2,128,128]{4,3,2,1,0:T(8,128)(2,1)}) conditional(s32[]{:T(128)} %bitcast.26, (bf16[32,256,128]{2,1,0:T(8,128)(2,1)}, bf16[32,256,128]{2,1,0:T(8,128)(2,1)S(1)}, bf16[1,64,256,128]{3,2,1,0:T(8,128)(2,1)}, s32[8,128]{1,0:T(8,128)S(1)}, s32[4,16,128]{2,1,0:T(8,128)S(1)}, ...), branch_computations={%region_0.0_spmd, %region_1.0_spmd, %region_2.0_spmd, %region_3.0_... | conditional | bytes 16777280 | solution.py:755
  13.9 96.8 %gather_panels_2.1 = (bf16[137,256,128]{2,1,0:T(8,128)(2,1)S(1)}, bf16[1,4,64,256,128]{4,3,2,1,0:T(8,128)(2,1)S(1)}, s32[16,128]{1,0:T(8,128)}) custom-call(bf16[32,256,128]{2,1,0:T(8,128)(2,1)} %get-tuple-element.147.left, bf16[32,256,128]{2,1,0:T(8,128)(2,1)S(1)} %get-tuple-element.148.own_left, bf16[1,64,256,128]{3,2,1,0:T(8,128)(2,1)} %get-tuple-element.149.right, ...), custom_call_target="tpu_custom_call" | custom-call | tf_op jit(solution)/shard_map/cond/branch_2_fun/gather_panels_2/pallas_call | solution.py:704
  110.7 7.3 %pair_products.10 = bf16[128,256,128]{2,1,0:T(8,128)(2,1)} custom-call(bf16[137,256,128]{2,1,0:T(8,128)(2,1)S(1)} %get-tuple-element.154.left, bf16[256,256,128]{2,1,0:T(8,128)(2,1)S(1)} %bitcast.34, s32[16,128]{1,0:T(8,128)} %get-tuple-element.156.order), custom_call_target="tpu_custom_call" | custom-call | tf_op jit(solution)/shard_map/cond/branch_2_fun/pair_products/pallas_call | solution.py:733

commit v2 on v1

--- a/solution.py
+++ b/solution.py
@@ -19,13 +19,16 @@
 
 
 def variants(slots, n_col, right_slots):
-    main, head = slots * 18 // 32, slots * 27 // 32
-    middle, rights = slots * 30 // 32, right_slots * 56 // 64
     scale = slots * (n_col - 1) / 96
-    found = [
-        (main, max(1, int(spill * scale)), head, middle, rights) for spill in (5, 7, 9, 11, 13, 16)
-    ]
-    found.append((main, max(1, int(24 * scale)), slots, slots, right_slots))
+    found = []
+    for spill, head, middle, rights in (
+        (5, 25, 28, 52), (7, 26, 28, 54), (9, 26, 29, 54), (11, 26, 30, 56), (13, 27, 30, 56),
+        (16, 28, 30, 58), (24, 32, 32, 64),
+    ):
+        found.append((
+            slots * 18 // 32, max(1, int(spill * scale)), slots * head // 32,
+            slots * middle // 32, right_slots * rights // 64,
+        ))
     return found + [(slots, 0, slots, slots, right_slots)]
 
 
@@ -486,7 +489,7 @@
     staged.start()
     pack_left(cuts[0][1], middle)
     for cut in range(1, len(cuts)):
-        if cuts[cut][2] != "rest":
+        if cuts[cut][2] == "main":
             start_left(0, cut)
 
     staged.wait()
@@ -532,27 +535,7 @@
 
                 spill_copy(up).start()
 
-    heads = (n_col - 2) * head
-    jobs = [(7, take_order)]
-    if spill:
-        jobs.append((heads + 0.02, send_spill))
-    for cut, (low, high, kind) in enumerate(cuts):
-        if kind == "rest":
-            jobs.append(((n_col - 3) * head + 0.03, functools.partial(start_left, 0, cut)))
-        for step in range(n_col - 1 if kind == "main" else n_col - 2):
-            when = step * head + high
-            if kind == "rest":
-                when = heads + (step + 1) * (high - low) + 0.04
-            jobs.append((when, functools.partial(take_left, step, cut)))
-    for step in range(1, n_chip):
-        for cut in range(RIGHT_CUTS):
-            when = ((step - 1) * RIGHT_CUTS + cut + 1) * limit * sets / RIGHT_CUTS + 0.5
-            jobs.append((when, functools.partial(take_right, step, cut)))
-    for _, job in sorted(jobs, key=lambda entry: entry[0]):
-        job()
-
-    kept.wait()
-    if head > main:
+    def take_sides():
         for step in range(1, n_col):
             for panel, there in (
                 (col - step, (col - step >= 0) & (col < n_col - 1)),
@@ -564,6 +547,33 @@
                     def _(at):
                         left_all[panel * slots + at] = side[panel * slots + at]
 
+    mains, heads = (n_col - 2) * main, (n_col - 2) * head
+    jobs = [(7, take_order)]
+    if spill:
+        jobs.append((heads + 0.02, send_spill))
+    if head > main:
+        jobs.append((heads + 0.03, take_sides))
+    for cut, (low, high, kind) in enumerate(cuts):
+        start = functools.partial(start_left, 0, cut)
+        if kind == "side":
+            jobs.append(((n_col - 3) * main + 0.01, start))
+        elif kind == "rest":
+            jobs.append((mains + (n_col - 3) * (head - main) + 0.01, start))
+        for step in range(n_col - 1 if kind == "main" else n_col - 2):
+            when = step * main + high
+            if kind == "side":
+                when = mains + (step + 1) * (high - low)
+            elif kind == "rest":
+                when = heads + (step + 1) * (high - low) + 0.04
+            jobs.append((when, functools.partial(take_left, step, cut)))
+    for step in range(1, n_chip):
+        for cut in range(RIGHT_CUTS):
+            when = ((step - 1) * RIGHT_CUTS + cut + 1) * limit * sets / RIGHT_CUTS + 2
+            jobs.append((when, functools.partial(take_right, step, cut)))
+    for _, job in sorted(jobs, key=lambda entry: entry[0]):
+        job()
+
+    kept.wait()
     if spill:
         for up in (False, True):
             pl.when(col == (n_col - 1 if up else 0))(spill_copy(up).wait_recv)

time: 119 us -> 115 us (0.966); the launches traced: 119 us -> 113 us
  Pallas kernels: 117 us -> 112 us
    pallas_call x1, Pallas kernels: 96.8 us -> 90.9 us  [run(): pl.pallas_call(functools.partial(gather_kernel, sizes, options[at]), out_...]
where the time goes in v2:
time: 115 us; the launch traced here: 113 us
  Pallas kernels  112 us (97%)
    pallas_call x1, Pallas kernels, run(): pl.pallas_call(functools.partial(gather_kernel, sizes, options[at]), out_...  90.9 us
    pallas_call x1, Pallas kernels, body(): pl.pallas_call(functools.partial(plan_kernel, (n_kpt,) + sizes[:-1], opti...  13.2 us
    pallas_call x1, Pallas kernels, run(): pl.pallas_call(functools.partial(product_kernel, sizes), out_shape=jax.Sh...  8.02 us

profile of v2, /device:TPU:0, one launch (start us, length us, event | category | flops | bytes accessed | tf_op | source)
XLA Modules:
  0.0 113.2 jit_solution(690924631769618122)
XLA Ops:
  0.0 13.2 %plan.1 = (bf16[32,256,128]{2,1,0:T(8,128)(2,1)S(1)}, s32[4,16,128]{2,1,0:T(8,128)S(1)}, s32[4,16,128]{2,1,0:T(8,128)S(1)}, s32[32,4,128]{2,1,0:T(4,128)S(1)}, s32[8,128]{1,0:T(8,128)S(1)}, /*index=5*/s32[1]{0:T(128)}) custom-call(bf16[32,256,128]{2,1,0:T(8,128)(2,1)} %bitcast.48, s32[2,16]{1,0:T(2,128)} %bitcast.67, s32[2,16]{1,0:T(2,128)} %bitcast.68, ...), custom_call_target="tpu_custom_call" | custom-call | tf_op jit(solution)/shard_map/plan/pallas_call | solution.py:679
  13.9 99.2 %conditional.1 = (bf16[8,16,2,128,128]{4,3,2,1,0:T(8,128)(2,1)}) conditional(s32[]{:T(128)} %bitcast.26, (bf16[32,256,128]{2,1,0:T(8,128)(2,1)}, bf16[32,256,128]{2,1,0:T(8,128)(2,1)S(1)}, bf16[1,64,256,128]{3,2,1,0:T(8,128)(2,1)}, s32[8,128]{1,0:T(8,128)S(1)}, s32[4,16,128]{2,1,0:T(8,128)S(1)}, ...), branch_computations={%region_0.0_spmd, %region_1.0_spmd, %region_2.0_spmd, %region_3.0_... | conditional | bytes 16777280 | solution.py:765
  13.9 90.9 %gather_panels_1.1 = (bf16[135,256,128]{2,1,0:T(8,128)(2,1)S(1)}, bf16[1,4,64,256,128]{4,3,2,1,0:T(8,128)(2,1)S(1)}, s32[16,128]{1,0:T(8,128)}) custom-call(bf16[32,256,128]{2,1,0:T(8,128)(2,1)} %get-tuple-element.137.left, bf16[32,256,128]{2,1,0:T(8,128)(2,1)S(1)} %get-tuple-element.138.own_left, bf16[1,64,256,128]{3,2,1,0:T(8,128)(2,1)} %get-tuple-element.139.right, ...), custom_call_target="tpu_custom_call" | custom-call | tf_op jit(solution)/shard_map/cond/branch_1_fun/gather_panels_1/pallas_call | solution.py:714
  104.8 8.0 %pair_products.9 = bf16[128,256,128]{2,1,0:T(8,128)(2,1)} custom-call(bf16[135,256,128]{2,1,0:T(8,128)(2,1)S(1)} %get-tuple-element.144.left, bf16[256,256,128]{2,1,0:T(8,128)(2,1)S(1)} %bitcast.33, s32[16,128]{1,0:T(8,128)} %get-tuple-element.146.order), custom_call_target="tpu_custom_call" | custom-call | tf_op jit(solution)/shard_map/cond/branch_1_fun/pair_products/pallas_call | solution.py:743

commit v3 on v2

--- a/solution.py
+++ b/solution.py
@@ -11,19 +11,21 @@
 LEVEL_CUT = 7
 DEAD = -1000
 GROUP = 24
+LEAD = 3
 MAIN_CUTS = 2
 RIGHT_CUTS = 8
-VMEM_BYTES = 62 * 1024 * 1024
+VMEM_BYTES = 59 * 1024 * 1024
 MESH = pl.DeviceIdType.MESH
 FAR = 2.0 ** 17
+FIRST = 1000
 
 
 def variants(slots, n_col, right_slots):
     scale = slots * (n_col - 1) / 96
     found = []
     for spill, head, middle, rights in (
-        (5, 25, 28, 52), (7, 26, 28, 54), (9, 26, 29, 54), (11, 26, 30, 56), (13, 27, 30, 56),
-        (16, 28, 30, 58), (24, 32, 32, 64),
+        (5, 25, 28, 52), (6, 25, 28, 52), (7, 26, 28, 54), (8, 26, 29, 54), (9, 26, 29, 54),
+        (10, 26, 29, 55), (12, 27, 30, 56), (14, 27, 30, 56), (18, 28, 30, 58), (24, 32, 32, 64),
     ):
         found.append((
             slots * 18 // 32, max(1, int(spill * scale)), slots * head // 32,
@@ -42,10 +44,12 @@
             levels[m:m + 1] + end >= LEVEL_CUT, 0.0,
             jnp.where(levels[m:m + 1] + union >= LEVEL_CUT, 1.0, 2.0),
         )
-        key = jnp.where(lane_row < per, kind * 128.0 + lane_row * ma + m, 1024.0)
-        rows.append(key)
+        level = levels[m:m + 1].astype(jnp.float32)
+        key = jnp.where(level >= FIRST / 2, -level, kind * 128.0 + lane_row * ma + m)
+        rows.append(jnp.where(lane_row < per, key, 1024.0))
         columns.append(jnp.sum(
-            jnp.where(lane == line, jnp.broadcast_to(key, (per, 128)), 0.0), axis=1, keepdims=True
+            jnp.where(lane == line, jnp.broadcast_to(rows[-1], (per, 128)), 0.0),
+            axis=1, keepdims=True,
         ))
     return rows, columns
 
@@ -71,8 +75,8 @@
 def plan_kernel(
     sizes, options, left,
     left_level, left_rows, left_count, right_level, right_cols, right_count,
-    own_left, left_meta, right_meta, tiles, perm, choice,
-    tile, meta, send, recv, lm_send, lm_recv, rm_send, rm_recv, left_sem,
+    own_left, lead_down, lead_up, left_meta, right_meta, tiles, perm, choice,
+    lead, tile, meta, send, recv, lead_send, lead_recv, lm_send, lm_recv, rm_send, rm_recv, left_sem,
 ):
     n_kpt, n_row, n_col, sets, per, ma, mb = sizes
     slots = per * ma
@@ -107,6 +111,20 @@
     live = lax.broadcasted_iota(jnp.int32, (ma, per), 0) < left_count[...]
     levels = jnp.where(live, left_level[...], DEAD)
     tile[:ma, :per] = levels
+    lane = lax.broadcasted_iota(jnp.int32, (per, 128), 1)
+    line = lax.broadcasted_iota(jnp.int32, (per, 128), 0)
+    keys, columns, ranks = [], [], []
+    for m in range(ma):
+        key = 256 * (8 - tile[m:m + 1, :]) + lane[:1] * ma + m
+        keys.append(jnp.where(lane[:1] < per, key, 1024 ** 2))
+        wide = jnp.broadcast_to(keys[-1], (per, 128))
+        columns.append(jnp.sum(jnp.where(lane == line, wide, 0), axis=1, keepdims=True))
+    for m in range(ma):
+        before = [jnp.where(key < keys[m], 1, 0) for key in columns]
+        rank = jnp.sum(functools.reduce(jnp.add, before), axis=0, keepdims=True)
+        ranks.append(jnp.where(lane[:1] < per, rank, slots))
+        tile[m:m + 1, :] = jnp.where(ranks[-1] < LEAD, FIRST - ranks[-1], tile[m:m + 1, :])
+    marked = tile[:ma, :]
     rights = []
     for which in range(sets):
         live = lax.broadcasted_iota(jnp.int32, (mb, per), 0) < right_count[which]
@@ -116,7 +134,9 @@
         tile[ma + which:ma + which + 1, 127:] = size.astype(jnp.int32)
     tiles[me] = tile[...]
     meta[...] = jnp.full(meta.shape, DEAD, jnp.int32)
-    meta[:ma, :per] = levels
+    meta[:ma, :] = marked
+    tail = 2 * ma + 2 * mb * sets
+    meta[tail:tail + ma, :per] = levels
     meta[ma:2 * ma, :per] = left_rows[...]
     for which in range(sets):
         base = 2 * ma + which * 2 * mb
@@ -124,6 +144,19 @@
         meta[base + mb:base + 2 * mb, :per] = rights[which]
     left_meta[col] = meta[...]
     right_meta[row] = meta[...]
+    stages[0].wait()
+    for at in range(LEAD):
+        spots = [jnp.where(rank == at, lane[:1] * ma + m, 0) for m, rank in enumerate(ranks)]
+        spot = jnp.max(functools.reduce(jnp.maximum, spots))
+        lead[at] = own_left[jnp.minimum(jnp.maximum(spot, 0), slots - 1)]
+
+    def lead_copy(up):
+        return pltpu.make_async_remote_copy(
+            src_ref=lead, dst_ref=lead_up if up else lead_down,
+            send_sem=lead_send.at[int(up)], recv_sem=lead_recv.at[int(up)],
+            device_id={"col": col + 1 if up else col - 1}, device_id_type=MESH,
+        )
+
     pl.semaphore_wait(barrier, total - 1)
 
     @pl.loop(1, total)
@@ -146,6 +179,8 @@
 
     for copy in meta_copies():
         copy.start()
+    for up in (False, True):
+        pl.when(col + 1 < n_col if up else col > 0)(lead_copy(up).start)
 
     @pl.loop(1, total)
     def _(step):
@@ -251,8 +286,9 @@
 
     for copy in meta_copies():
         copy.wait()
-    for copy in stages:
-        copy.wait()
+    for up in (False, True):
+        pl.when(col + 1 < n_col if up else col > 0)(lead_copy(up).wait_send)
+        pl.when(col > 0 if up else col + 1 < n_col)(lead_copy(up).wait_recv)
 
     @pl.loop(1, total)
     def _(step):
@@ -308,7 +344,9 @@
             values = pltpu.roll(values, panel * per, 1) if panel else values
             return jnp.where(here, values, 0.0)
 
-        lefts = lefts + moved(left_meta[panel, :2 * ma, :].astype(jnp.float32))
+        tail = 2 * ma + 2 * mb * sets
+        left = [left_meta[panel, tail:tail + ma, :], left_meta[panel, ma:2 * ma, :]]
+        lefts = lefts + moved(jnp.concatenate(left, axis=0).astype(jnp.float32))
         right = right_meta[panel % n_row, base:base + 2 * mb, :].astype(jnp.float32)
         rights = rights + moved(right)
         places = places + moved(found)
@@ -374,7 +412,7 @@
 
 
 def gather_kernel(
-    sizes, option, left, own_left, right, perm, left_meta, right_meta, tiles,
+    sizes, option, left, own_left, lead_down, lead_up, right, perm, left_meta, right_meta, tiles,
     left_all, right_all, order,
     own_right, packed_down, packed_up, side, spill_down, spill_up,
     up_send, up_recv, down_send, down_recv, spill_send, spill_recv,
@@ -403,8 +441,9 @@
     kept = pltpu.make_async_copy(left, left_all.at[pl.ds(col * slots, slots)], left_sem)
     kept.start()
 
-    bounds = [main * at // MAIN_CUTS for at in range(MAIN_CUTS + 1)]
+    bounds = [LEAD + (main - LEAD) * at // MAIN_CUTS for at in range(MAIN_CUTS + 1)]
     cuts = [(low, high, "main") for low, high in zip(bounds, bounds[1:])]
+    cuts.append((0, LEAD, "lead"))
     if head > main:
         cuts.append((main, head, "side"))
     if middle > head:
@@ -418,21 +457,23 @@
         span = pl.ds(panel * slots + low, high - low)
         target = side.at[span] if kind == "side" else left_all.at[span]
         source = (packed_up if up else packed_down).at[pl.ds(low, high - low)]
+        if kind == "lead" and step == 1:
+            source = lead_up if up else lead_down
         send, recv = (up_send, up_recv) if up else (down_send, down_recv)
         return pltpu.make_async_remote_copy(
-            src_ref=source if step == 0 else target, dst_ref=target,
+            src_ref=source if step == int(kind == "lead") else target, dst_ref=target,
             send_sem=send.at[step, cut], recv_sem=recv.at[step, cut],
             device_id={"col": col + 1 if up else col - 1}, device_id_type=MESH,
         )
 
     def left_sends(step, cut, up):
-        mid = 0 if cuts[cut][2] == "main" else 1
+        mid = 0 if cuts[cut][2] in ("main", "lead") else 1
         if up:
             return (col + 1 < n_col - mid) & (col - step >= 0)
         return (col - 1 >= mid) & (col + step < n_col)
 
     def left_receives(step, cut, up):
-        mid = 0 if cuts[cut][2] == "main" else 1
+        mid = 0 if cuts[cut][2] in ("main", "lead") else 1
         if up:
             return (col - 1 - step >= 0) & (col < n_col - mid)
         return (col + 1 + step < n_col) & (col >= mid)
@@ -440,6 +481,11 @@
     def start_left(step, cut):
         for up in (True, False):
             pl.when(left_sends(step, cut, up))(left_copy(step, cut, up).start)
+
+    def steps_of(kind):
+        if kind == "lead":
+            return range(1, n_col - 1)
+        return range(n_col - 1 if kind == "main" else n_col - 2)
 
     def spill_copy(up):
         return pltpu.make_async_remote_copy(
@@ -491,6 +537,8 @@
     for cut in range(1, len(cuts)):
         if cuts[cut][2] == "main":
             start_left(0, cut)
+        elif cuts[cut][2] == "lead" and n_col > 2:
+            start_left(1, cut)
 
     staged.wait()
     for which in range(sets):
@@ -519,6 +567,14 @@
         passed(step, cut).start()
 
     def take_order():
+        for panel, there, found in (
+            (col + 1, col + 1 < n_col, lead_down), (col - 1, col > 0, lead_up)
+        ):
+            @pl.when(there)
+            def _():
+                for at in range(LEAD):
+                    left_all[panel * slots + at] = found[at]
+
         order_pairs(
             sizes, main, lax.axis_index("kpt"), col, tiles, left_meta, right_meta, order
         )
@@ -547,7 +603,7 @@
                     def _(at):
                         left_all[panel * slots + at] = side[panel * slots + at]
 
-    mains, heads = (n_col - 2) * main, (n_col - 2) * head
+    mains, heads = (n_col - 2) * main - LEAD, (n_col - 2) * head - LEAD
     jobs = [(7, take_order)]
     if spill:
         jobs.append((heads + 0.02, send_spill))
@@ -556,11 +612,11 @@
     for cut, (low, high, kind) in enumerate(cuts):
         start = functools.partial(start_left, 0, cut)
         if kind == "side":
-            jobs.append(((n_col - 3) * main + 0.01, start))
+            jobs.append(((n_col - 3) * main - LEAD + 0.01, start))
         elif kind == "rest":
             jobs.append((mains + (n_col - 3) * (head - main) + 0.01, start))
-        for step in range(n_col - 1 if kind == "main" else n_col - 2):
-            when = step * main + high
+        for step in steps_of(kind):
+            when = step * main + high - LEAD
             if kind == "side":
                 when = mains + (step + 1) * (high - low)
             elif kind == "rest":
@@ -584,7 +640,7 @@
             across(step, cut).wait_send()
             passed(step, cut).wait()
     for cut, entry in enumerate(cuts):
-        for step in range(n_col - 1 if entry[2] == "main" else n_col - 2):
+        for step in steps_of(entry[2]):
             for up in (True, False):
                 pl.when(left_sends(step, cut, up))(left_copy(step, cut, up).wait_send)
 
@@ -673,13 +729,14 @@
     options = variants(slots, n_col, per * mb)
     sizes = (n_row, n_col, sets, per, ma, mb, n_row * sets * per // n_col)
     tile_rows = -(-(ma + sets) // 4) * 4
-    meta_rows = -(-(2 * ma + 2 * mb * sets) // 8) * 8
+    meta_rows = -(-(3 * ma + 2 * mb * sets) // 8) * 8
     lines = -(-n_col * per * ma * mb // 128)
     order_rows = -(-(2 * lines + 3) // 8) * 8
-    own_left, left_meta, right_meta, tiles, perm, choice = pl.pallas_call(
+    own_left, lead_down, lead_up, left_meta, right_meta, tiles, perm, choice = pl.pallas_call(
         functools.partial(plan_kernel, (n_kpt,) + sizes[:-1], options),
         out_shape=(
             pltpu.VMEM(left.shape, left.dtype),
+            *[pltpu.VMEM((LEAD,) + left.shape[1:], left.dtype)] * 2,
             jax.ShapeDtypeStruct((n_col, meta_rows, 128), jnp.int32),
             jax.ShapeDtypeStruct((n_row, meta_rows, 128), jnp.int32),
             jax.ShapeDtypeStruct((total, tile_rows, 128), jnp.int32),
@@ -687,11 +744,13 @@
             jax.ShapeDtypeStruct((1,), jnp.int32),
         ),
         in_specs=[any_space] + [vmem] * 6,
-        out_specs=(vmem,) * 5 + (smem,),
+        out_specs=(vmem,) * 7 + (smem,),
         scratch_shapes=[
+            pltpu.VMEM((LEAD,) + left.shape[1:], left.dtype),
             pltpu.VMEM((tile_rows, 128), jnp.int32),
             pltpu.VMEM((meta_rows, 128), jnp.int32),
             *[dma((total,))] * 2,
+            *[dma((2,))] * 2,
             *[dma((n_col - 1,))] * 2,
             *[dma((n_row - 1,))] * 2,
             dma,
@@ -706,11 +765,12 @@
 
     kb_cols = sizes[-1]
     right_shape = (sets, n_row) + right.shape[1:]
-    most = (n_col + 1) * left.size + n_row * right.size + 24 * left.size // slots
+    assert LEAD <= per
+    most = (n_col + 1) * left.size + 2 * LEAD * left.size // slots + n_row * right.size + 24 * left.size // slots
     limit = VMEM_BYTES - most * left.dtype.itemsize
 
-    def run(at, left, own_left, right, perm, left_meta, right_meta, tiles):
-        cuts, spill = MAIN_CUTS + 2, max(options[at][1], 1)
+    def run(at, left, own_left, lead_down, lead_up, right, perm, left_meta, right_meta, tiles):
+        cuts, spill = MAIN_CUTS + 3, max(options[at][1], 1)
         left_all, right_all, order = pl.pallas_call(
             functools.partial(gather_kernel, sizes, options[at]),
             out_shape=(
@@ -718,7 +778,7 @@
                 pltpu.VMEM(right_shape, right.dtype),
                 jax.ShapeDtypeStruct((order_rows, 128), jnp.int32),
             ),
-            in_specs=[any_space, vmem, any_space, smem, vmem, vmem, vmem],
+            in_specs=[any_space, vmem, vmem, vmem, any_space, smem, vmem, vmem, vmem],
             out_specs=(vmem, vmem, vmem),
             scratch_shapes=[
                 pltpu.VMEM(right.shape, right.dtype),
@@ -738,6 +798,8 @@
             name=f"gather_panels_{at}",
         )(
             left, pltpu.with_memory_space_constraint(own_left, pltpu.VMEM),
+            pltpu.with_memory_space_constraint(lead_down, pltpu.VMEM),
+            pltpu.with_memory_space_constraint(lead_up, pltpu.VMEM),
             right, perm, left_meta, right_meta, tiles,
         )
         return pl.pallas_call(
@@ -764,7 +826,7 @@
 
     out = lax.switch(
         choice[0], [functools.partial(run, at) for at in range(len(options))],
-        left, own_left, right, perm, left_meta, right_meta, tiles,
+        left, own_left, lead_down, lead_up, right, perm, left_meta, right_meta, tiles,
     )
     return out.reshape(GR, kb_cols, 2, width, width)
 

time: 115 us -> 114 us (level); the launches traced: 113 us -> 115 us
  Pallas kernels: 112 us -> 114 us
    pallas_call x1, Pallas kernels: 13.2 us -> 16.5 us  [body(): pl.pallas_call(functools.partial(plan_kernel, (n_kpt,) + sizes[:-1], opti...]
    pallas_call x1, Pallas kernels: 90.9 us -> 89.3 us  [run(): pl.pallas_call(functools.partial(gather_kernel, sizes, options[at]), out_...]
where the time goes in v3:
time: 114 us; the launch traced here: 115 us
  Pallas kernels  114 us (100%)
    pallas_call x1, Pallas kernels, run(): pl.pallas_call(functools.partial(gather_kernel, sizes, options[at]), out_...  89.3 us
    pallas_call x1, Pallas kernels, body(): pl.pallas_call(functools.partial(plan_kernel, (n_kpt,) + sizes[:-1], opti...  16.5 us
    pallas_call x1, Pallas kernels, run(): pl.pallas_call(functools.partial(product_kernel, sizes), out_shape=jax.Sh...  8.41 us

profile of v3, /device:TPU:0, one launch (start us, length us, event | category | flops | bytes accessed | tf_op | source)
XLA Modules:
  0.0 115.2 jit_solution(2250920727906227280)
XLA Ops:
  0.0 16.5 %plan.1 = (bf16[32,256,128]{2,1,0:T(8,128)(2,1)S(1)}, bf16[3,256,128]{2,1,0:T(8,128)(2,1)S(1)}, bf16[3,256,128]{2,1,0:T(8,128)(2,1)S(1)}, s32[4,16,128]{2,1,0:T(...) custom-call(bf16[32,256,128]{2,1,0:T(8,128)(2,1)} %bitcast.60, ...), custom_call_target="tpu_custom_call" | custom-call | tf_op jit(solution)/shard_map/plan/pallas_call | solution.py:735
  17.1 98.0 %conditional.1 = (bf16[8,16,2,128,128]{4,3,2,1,0:T(8,128)(2,1)}) conditional(s32[]{:T(128)} %bitcast.32, (bf16[32,256,128]{2,1,0:T(8,128)(2,1)}, bf16[32,256,128]{2,1,0:T(8,128)(2,1)S(1)}, bf16[3,256,128]{2,1,0:T(8,128)(2,1)S(1)}, bf16[3,256,128]{2,1,0:T(8,128)(2,1)S(1)}, bf16[1,64,256,128]{3,2,1,0:T(8,128)(2,1)}, ...), branch_computations={%region_0.0_spmd, %region_1.0_spmd, %region_2.0_spmd, %region_3.0_... | conditional | bytes 8 | solution.py:827
  17.2 89.3 %gather_panels_4.1 = (bf16[137,256,128]{2,1,0:T(8,128)(2,1)S(1)}, bf16[1,4,64,256,128]{4,3,2,1,0:T(8,128)(2,1)S(1)}, s32[16,128]{1,0:T(8,128)}) custom-call(bf16[32,256,128]{2,1,0:T(8,128)(2,1)} %get-tuple-element.264.left, bf16[32,256,128]{2,1,0:T(8,128)(2,1)S(1)} %get-tuple-element.265.own_left, bf16[3,256,128]{2,1,0:T(8,128)(2,1)S(1)} %get-tuple-element.266.lead_down, ...), custom_call_target="tpu_custom_call" | custom-call | tf_op jit(solution)/shard_map/cond/branch_4_fun/gather_panels_4/pallas_call | solution.py:774
  106.5 8.4 %pair_products.15 = bf16[128,256,128]{2,1,0:T(8,128)(2,1)} custom-call(bf16[137,256,128]{2,1,0:T(8,128)(2,1)S(1)} %get-tuple-element.273.left, bf16[256,256,128]{2,1,0:T(8,128)(2,1)S(1)} %bitcast.42, s32[16,128]{1,0:T(8,128)} %get-tuple-element.275.order), custom_call_target="tpu_custom_call" | custom-call | tf_op jit(solution)/shard_map/cond/branch_4_fun/pair_products/pallas_call | solution.py:805

commit v4 on v3

--- a/solution.py
+++ b/solution.py
@@ -24,8 +24,8 @@
     scale = slots * (n_col - 1) / 96
     found = []
     for spill, head, middle, rights in (
-        (5, 25, 28, 52), (6, 25, 28, 52), (7, 26, 28, 54), (8, 26, 29, 54), (9, 26, 29, 54),
-        (10, 26, 29, 55), (12, 27, 30, 56), (14, 27, 30, 56), (18, 28, 30, 58), (24, 32, 32, 64),
+        (5, 26, 29, 54), (6, 26, 29, 55), (7, 26, 30, 56), (8, 26, 30, 56), (9, 26, 30, 58),
+        (10, 27, 31, 58), (12, 27, 31, 60), (14, 28, 32, 60), (18, 28, 32, 60), (24, 32, 32, 64),
     ):
         found.append((
             slots * 18 // 32, max(1, int(spill * scale)), slots * head // 32,
@@ -84,24 +84,33 @@
     total = n_kpt * n_row * n_col
     me = (kpt * n_row + row) * n_col + col
 
-    def place_of(step):
-        other = (me + step) % total
-        return {
-            "kpt": other // (n_row * n_col), "row": (other // n_col) % n_row, "col": other % n_col
-        }
-
-    def copy_of(step):
+    groups = n_kpt * n_row
+    group = kpt * n_row + row
+
+    def place_of(far, side):
+        other = (group + far) % groups
+        return {"kpt": other // n_row, "row": other % n_row, "col": (col + side) % n_col}
+
+    def copy_of(far, side):
+        at = far * n_col + side
         return pltpu.make_async_remote_copy(
-            src_ref=tile, dst_ref=tiles.at[me], send_sem=send.at[step], recv_sem=recv.at[step],
-            device_id=place_of(step), device_id_type=MESH,
-        )
+            src_ref=tile, dst_ref=tiles.at[me], send_sem=send.at[at], recv_sem=recv.at[at],
+            device_id=place_of(far, side), device_id_type=MESH,
+        )
+
+    def for_others(act):
+        @pl.loop(1, groups)
+        def _(far):
+            for side in range(n_col):
+                act(far, side)
+
+        for side in range(1, n_col):
+            act(0, side)
 
     barrier = pltpu.get_barrier_semaphore()
-
-    @pl.loop(1, total)
-    def _(step):
-        pl.semaphore_signal(barrier, inc=1, device_id=place_of(step), device_id_type=MESH)
-
+    for_others(lambda far, side: pl.semaphore_signal(
+        barrier, inc=1, device_id=place_of(far, side), device_id_type=MESH
+    ))
     stages = (
         pltpu.make_async_copy(left, own_left, left_sem),
     )
@@ -159,9 +168,7 @@
 
     pl.semaphore_wait(barrier, total - 1)
 
-    @pl.loop(1, total)
-    def _(step):
-        copy_of(step).start()
+    for_others(lambda far, side: copy_of(far, side).start())
 
     def meta_copies():
         for step in range(1, n_col):
@@ -182,9 +189,7 @@
     for up in (False, True):
         pl.when(col + 1 < n_col if up else col > 0)(lead_copy(up).start)
 
-    @pl.loop(1, total)
-    def _(step):
-        copy_of(step).wait_recv()
+    for_others(lambda far, side: copy_of(far, side).wait_recv())
 
     def at_device(k, r, c):
         return (k * n_row + r) * n_col + c
@@ -290,9 +295,7 @@
         pl.when(col + 1 < n_col if up else col > 0)(lead_copy(up).wait_send)
         pl.when(col > 0 if up else col + 1 < n_col)(lead_copy(up).wait_recv)
 
-    @pl.loop(1, total)
-    def _(step):
-        copy_of(step).wait_send()
+    for_others(lambda far, side: copy_of(far, side).wait_send())
 
 
 def order_pairs(sizes, main, kpt, col, tiles, left_meta, right_meta, order):

time: 114 us -> 115 us (level)
    pallas_call x1, Pallas kernels: 89.3 us -> 90.7 us  [run(): pl.pallas_call(functools.partial(gather_kernel, sizes, options[at]), out_...]
where the time goes in v4:
time: 115 us; the launch traced here: 116 us
  Pallas kernels  115 us (100%)
    pallas_call x1, Pallas kernels, run(): pl.pallas_call(functools.partial(gather_kernel, sizes, options[at]), out_...  90.7 us
    pallas_call x1, Pallas kernels, body(): pl.pallas_call(functools.partial(plan_kernel, (n_kpt,) + sizes[:-1], opti...  16.3 us
    pallas_call x1, Pallas kernels, run(): pl.pallas_call(functools.partial(product_kernel, sizes), out_shape=jax.Sh...  8.06 us

profile of v4, /device:TPU:0, one launch (start us, length us, event | category | flops | bytes accessed | tf_op | source)
XLA Modules:
  0.0 116.2 jit_solution(9313682269665245736)
XLA Ops:
  0.0 16.3 %plan.1 = (bf16[32,256,128]{2,1,0:T(8,128)(2,1)S(1)}, bf16[3,256,128]{2,1,0:T(8,128)(2,1)S(1)}, bf16[3,256,128]{2,1,0:T(8,128)(2,1)S(1)}, s32[4,16,128]{2,1,0:T(...) custom-call(bf16[32,256,128]{2,1,0:T(8,128)(2,1)} %bitcast.60, ...), custom_call_target="tpu_custom_call" | custom-call | tf_op jit(solution)/shard_map/plan/pallas_call | solution.py:738
  17.0 99.0 %conditional.1 = (bf16[8,16,2,128,128]{4,3,2,1,0:T(8,128)(2,1)}) conditional(s32[]{:T(128)} %bitcast.32, (bf16[32,256,128]{2,1,0:T(8,128)(2,1)}, bf16[32,256,128]{2,1,0:T(8,128)(2,1)S(1)}, bf16[3,256,128]{2,1,0:T(8,128)(2,1)S(1)}, bf16[3,256,128]{2,1,0:T(8,128)(2,1)S(1)}, bf16[1,64,256,128]{3,2,1,0:T(8,128)(2,1)}, ...), branch_computations={%region_0.0_spmd, %region_1.0_spmd, %region_2.0_spmd, %region_3.0_... | conditional | bytes 8 | solution.py:830
  17.2 90.7 %gather_panels_5.1 = (bf16[138,256,128]{2,1,0:T(8,128)(2,1)S(1)}, bf16[1,4,64,256,128]{4,3,2,1,0:T(8,128)(2,1)S(1)}, s32[16,128]{1,0:T(8,128)}) custom-call(bf16[32,256,128]{2,1,0:T(8,128)(2,1)} %get-tuple-element.276.left, bf16[32,256,128]{2,1,0:T(8,128)(2,1)S(1)} %get-tuple-element.277.own_left, bf16[3,256,128]{2,1,0:T(8,128)(2,1)S(1)} %get-tuple-element.278.lead_down, ...), custom_call_target="tpu_custom_call" | custom-call | tf_op jit(solution)/shard_map/cond/branch_5_fun/gather_panels_5/pallas_call | solution.py:777
  107.9 8.1 %pair_products.16 = bf16[128,256,128]{2,1,0:T(8,128)(2,1)} custom-call(bf16[138,256,128]{2,1,0:T(8,128)(2,1)S(1)} %get-tuple-element.285.left, bf16[256,256,128]{2,1,0:T(8,128)(2,1)S(1)} %bitcast.43, s32[16,128]{1,0:T(8,128)} %get-tuple-element.287.order), custom_call_target="tpu_custom_call" | custom-call | tf_op jit(solution)/shard_map/cond/branch_5_fun/pair_products/pallas_call | solution.py:808
